TPU v7x, 32 devices: a whole 2x2x4 slice. The times are simulated.
32 devices in a mesh: head: 4 (over z), outer: 4 (over x, core), inner: 2 (over y).
Axes of the slice: x: 2, y: 2, z: 4, core: 2. Of those that a mesh axis runs over, the one named last changes fastest.
Arguments:
- query_nope: bfloat16 [1024, 2048], P(('outer', 'inner'), 'head'), may hold values from -6 to 6
- query_rope: bfloat16 [1024, 1024], P(('outer', 'inner'), 'head'), may hold values from -8 to 8
- cache: bfloat16 [1024, 576], P(('outer', 'inner')), may hold values from -8 to 8
- span_ids: int32 [16], P(('outer', 'inner')), may hold values from 0 to 15, as said below
- key_up: bfloat16 [512, 2048], P(None, 'head'), may hold values from -0.25 to 0.25
- value_up: bfloat16 [512, 2048], P(None, 'head'), may hold values from -1.5 to 1.5
- out_proj: bfloat16 [2048, 2048], P('head'), may hold values from -1.1953125 to 1.1953125
Outputs:
- mixed: bfloat16 [1024, 2048], P(('outer', 'inner'), 'head')
Inputs may be any that keep to these rules, and one draw needn't show every extreme that they name: `span_ids`: each of 0 to 15 appears once; entries 2 r and 2 r + 1 belong to storage rows r * 128 to (r + 1) * 128 - 1.
All inputs are finite; a program needn't handle non-finite values.
Results may differ from a plain program's by a relative error of at most 0.014.
Values may be sent and summed in bfloat16 or wider, within the bound.
No kernel may reach another device: no remote copies, remote signals or barrier semaphores. Data moves between devices by JAX's collectives and lax.ppermute only.
A program may use at most 64 MiB of HBM per device.

v0:
```python
import math

import jax
import jax.numpy as jnp
from jax import lax
from jax.sharding import PartitionSpec as P

LATENT = 512
ROPE = 64
NOPE = 128
VDIM = 128
SPAN = 64


lowest_start = -1e30


def shards(query_nope, query_rope, cache, span_ids, key_up, value_up, out_proj):
    rows_dev = cache.shape[0]
    heads_dev = key_up.shape[1] // NOPE
    softmax_scale = (NOPE + ROPE) ** (-0.5)
    owners = lax.all_gather(span_ids, ("outer", "inner"), axis=0, tiled=True)
    span_count = owners.shape[0]
    offsets = jnp.arange(SPAN, dtype=jnp.int32)
    query_pos = (span_ids[:, None] * SPAN + offsets[None, :]).reshape(rows_dev)
    row_pos = jnp.tile(query_pos, heads_dev)
    query_heads = query_nope.reshape(rows_dev, heads_dev, NOPE)
    key_weight = key_up.reshape(LATENT, heads_dev, NOPE)
    q_latent = jnp.einsum(
        "shd,chd->hsc", query_heads, key_weight, preferred_element_type=jnp.float32
    ).astype(jnp.bfloat16)
    q_rotary = jnp.transpose(query_rope.reshape(rows_dev, heads_dev, ROPE), (1, 0, 2))
    queries = jnp.concatenate([q_latent, q_rotary], axis=2).reshape(
        heads_dev * rows_dev, LATENT + ROPE
    )
    span_slots = jnp.arange(span_count, dtype=jnp.int32)
    total_rows = heads_dev * rows_dev
    start_state = (
        jnp.full((total_rows,), lowest_start, jnp.float32),
        jnp.zeros((total_rows,), jnp.float32),
        jnp.zeros((total_rows, LATENT), jnp.float32),
    )
    group_rows = lax.all_gather(cache, "inner", axis=0, tiled=True)
    segment = lax.all_gather(group_rows, "outer", axis=0, tiled=True)
    length = segment.shape[0]
    seg_rows = jnp.arange(length, dtype=jnp.int32)
    seg_spans = seg_rows // SPAN
    span_now = jnp.sum(
        jnp.where(seg_spans[:, None] == span_slots[None, :], owners[None, :], 0), axis=1
    )
    key_pos = span_now * SPAN + seg_rows % SPAN
    block_rows = math.gcd(length, 2048)

    def one_block(step_index, status):
        running_max, running_sum, numerator = status
        key_block = lax.dynamic_slice_in_dim(segment, step_index * block_rows, block_rows, 0)
        block_pos = lax.dynamic_slice_in_dim(key_pos, step_index * block_rows, block_rows, 0)
        scores = (
            lax.dot_general(
                queries, key_block, (((1,), (1,)), ((), ())), preferred_element_type=jnp.float32
            )
            * softmax_scale
        )
        visible = block_pos[None, :] <= row_pos[:, None]
        scores = jnp.where(visible, scores, -jnp.inf)
        new_max = jnp.maximum(running_max, jnp.max(scores, axis=1))
        rescale = jnp.exp(running_max - new_max)
        weights = jnp.exp(scores - new_max[:, None])
        running_sum = running_sum * rescale + jnp.sum(weights, axis=1)
        numerator = numerator * rescale[:, None] + jnp.dot(
            weights.astype(jnp.bfloat16), key_block[:, :LATENT], preferred_element_type=jnp.float32
        )
        return (new_max, running_sum, numerator)

    result_state = lax.fori_loop(0, length // block_rows, one_block, start_state)
    running_sum = result_state[1]
    numerator = result_state[2]
    latent_out = (
        (numerator / running_sum[:, None]).astype(jnp.bfloat16).reshape(heads_dev, rows_dev, LATENT)
    )
    value_weight = value_up.reshape(LATENT, heads_dev, VDIM)
    head_out = jnp.einsum(
        "hsc,chd->shd", latent_out, value_weight, preferred_element_type=jnp.float32
    ).astype(jnp.bfloat16)
    head_out = head_out.reshape(rows_dev, heads_dev * VDIM)
    head_part = jnp.dot(head_out, out_proj, preferred_element_type=jnp.float32)
    return lax.psum_scatter(head_part.astype(jnp.bfloat16), "head", scatter_dimension=1, tiled=True)


def solution(mesh):
    return jax.shard_map(
        shards,
        mesh=mesh,
        in_specs=(
            P(("outer", "inner"), "head"),
            P(("outer", "inner"), "head"),
            P(("outer", "inner"), None),
            P(("outer", "inner")),
            P(None, "head"),
            P(None, "head"),
            P("head", None),
        ),
        out_specs=P(("outer", "inner"), "head"),
        check_vma=False,
    )
```

profile of v0, /device:TPU:0, one launch (start us, length us, event | category | flops | bytes accessed | tf_op | source)
XLA Modules:
  0.0 69.0 jit_solution(13893021611111289871)
XLA Ops:
  6.5 9.6 %all_gather.10 = bf16[256,576]{0,1:T(8,128)(2,1)} all-gather(bf16[128,576]{0,1:T(8,128)(2,1)} %param.9), channel_id=1, replica_groups=mesh['head'=4,'outer'=4,'inner'=2] {'inner'}, dimensions={0}, use_global_device_ids=true | all-gather | bytes 442368 | tf_op jit(solution)/shard_map/all_gather | solution.py:43
  16.1 0.0 all-gather.2.cloned.1.call-update
  16.2 0.0 reduce-scatter.2.cloned.1.call-start
  16.2 1.2 %dynamic-slice = u32[1]{0:T(128)} dynamic-slice(u32[32]{0:T(128)} %constant.58, u32[]{:T(128)S(6)} %add.71), dynamic_slice_sizes={1} | dynamic-slice | bytes 12
  18.1 0.9 %dynamic-update-slice = s32[16]{0:T(128)S(1)} dynamic-update-slice(s32[16]{0:T(128)S(1)} %broadcast.93, s32[2]{0:T(128)} %param.10, u32[]{:T(128)} %bitcast) | dynamic-update-slice | bytes 20
  19.0 7.4 %all-reduce = s32[16]{0:T(128)S(1)} all-reduce(s32[16]{0:T(128)S(1)} %dynamic-update-slice), channel_id=1, replica_groups=mesh['head'=4,'outer'=4,'inner'=2] {'outer','inner'}, use_global_device_ids=true, to_apply=%add | all-reduce | flops 16 | bytes 128
  26.3 0.9 %copy.18 = bf16[128,256]{0,1:T(8,128)(2,1)S(1)} copy(bf16[128,256]{1,0:T(8,128)(2,1)} %param.8) | data formatting | bytes 131072 | tf_op args[1]
  27.3 0.1 copy.19
  27.4 0.7 broadcast_multiply_fusion
  28.1 0.1 iota_add_fusion
  28.2 0.1 add.68
  28.3 1.3 %copy.21 = bf16[512,512]{0,1:T(8,128)(2,1)S(1)} copy(bf16[512,512]{1,0:T(8,128)(2,1)} %param.12) | data formatting | bytes 1048576 | tf_op jit(solution)/shard_map/reshape | solution.py:81
  29.5 0.1 select_reduce_fusion
  29.6 0.3 convolution_convert_fusion.1
  29.9 0.1 pad_maximum_fusion
  30.0 4.2 %all-gather.2.cloned.1.call-done = bf16[1024,576]{0,1:T(8,128)(2,1)} async-done(((bf16[256,576]{0,1:T(8,128)(2,1)}), bf16[1024,576]{0,1:T(8,128)(2,1)}) %all-gather.2.cloned.1.call-update) | async-done | bytes 1179664 | tf_op jit(solution)/shard_map/all_gather | solution.py:44
  34.3 2.4 %fusion.20 = (f32[512]{0:T(512)S(1)}, f32[512,1024]{1,0:T(8,128)S(1)}) fusion(bf16[512,576]{1,0:T(8,128)(2,1)S(1)} %bitcast.32, bf16[1024,576]{0,1:T(8,128)(2,1)} %all-gather.2.cloned.1.call-done, s32[512]{0:T(512)S(1)} %broadcast_bitcast_fusion, s32[1024]{0:T(1024)S(1)} %fusion.17), kind=kOutput, calls=%fused_computation.37 | convolution fusion | flops 606076416 | bytes 3874816 | tf_op jit(solution)/shard_map/while/body/eval_jaxpr/dot_general | solution.py:59
  36.7 0.5 fusion
  37.2 0.7 %copy-done.3 = bf16[1024,576]{0,1:T(8,128)(2,1)S(1)} copy-done((bf16[1024,576]{0,1:T(8,128)(2,1)S(1)}, bf16[1024,576]{0,1:T(8,128)(2,1)}, u32[]{:S(2)}) %copy-start.3) | copy-done | bytes 1179672
  37.9 0.8 %fusion.3 = bf16[512,512]{1,0:T(8,128)(2,1)S(1)} fusion(f32[512,1024]{1,0:T(8,128)S(1)} %get-tuple-element.24, bf16[1024,576]{0,1:T(8,128)(2,1)S(1)} %copy-done.3, f32[512]{0:T(512)S(1)} %broadcast_maximum_fusion, f32[512]{0:T(512)S(1)} %get-tuple-element.22, f32[512]{0:T(512)S(1)} %get-tuple-element.21), kind=kOutput, calls=%fused_computation.8 | convolution fusion | flops 538705920 | bytes 3676160 | tf_op jit(solution)/shard_map/while/body/eval_jaxpr/dot_general | solution.py:70
  38.7 0.3 convolution_convert_fusion.2
  39.0 1.3 %convolution_convert_fusion = bf16[128,2048]{1,0:T(8,128)(2,1)} fusion(bf16[128,512]{0,1:T(8,128)(2,1)S(1)} %bitcast.35, bf16[512,2048]{1,0:T(8,128)(2,1)S(1)} %copy-done), kind=kOutput, calls=%fused_computation | convolution fusion | flops 268697600 | bytes 2752512 | tf_op jit(solution)/shard_map/dot_general | solution.py:86
  40.3 0.0 reduce-scatter.2.cloned.1.call-update
  40.3 21.9 %reduce-scatter.2.cloned.1.call-done = bf16[128,512]{1,0:T(8,128)(2,1)} async-done(((bf16[128,2048]{1,0:T(8,128)(2,1)}), bf16[128,512]{1,0:T(8,128)(2,1)}) %reduce-scatter.2.cloned.1.call-update) | async-done | bytes 131088 | tf_op jit(solution)/shard_map/reduce_scatter | solution.py:87
  (14 shorter events, 0.0 us)
Async XLA Ops:
  6.5 32.5 %copy-start = (bf16[512,2048]{1,0:T(8,128)(2,1)S(1)}, bf16[512,2048]{1,0:T(8,128)(2,1)}, u32[]{:S(2)}) copy-start(bf16[512,2048]{1,0:T(8,128)(2,1)} %param.13) | copy-start | bytes 6291460
  6.5 23.1 %copy-start.1 = (bf16[512,512]{1,0:T(8,128)(2,1)S(1)}, bf16[512,512]{1,0:T(8,128)(2,1)}, u32[]{:S(2)}) copy-start(bf16[512,512]{1,0:T(8,128)(2,1)} %param.11) | copy-start | bytes 1572868
  6.5 23.1 %copy-start.2 = (bf16[128,512]{1,0:T(8,128)(2,1)S(1)}, bf16[128,512]{1,0:T(8,128)(2,1)}, u32[]{:S(2)}) copy-start(bf16[128,512]{1,0:T(8,128)(2,1)} %param.7) | copy-start | bytes 393220
  6.5 27.7 %all-gather.2.cloned.1.call-start = ((), (), s32[]{:S(2)}) async-start(), calls=%async_computation.1 | async-start | bytes 1474560 | tf_op jit(solution)/shard_map/all_gather | solution.py:44
  16.2 46.0 %reduce-scatter.2.cloned.1.call-start = ((), (), s32[]{:S(2)}) async-start(), calls=%async_computation.2 | async-start | bytes 655360 | tf_op jit(solution)/shard_map/reduce_scatter | solution.py:87
  36.7 1.3 %copy-start.3 = (bf16[1024,576]{0,1:T(8,128)(2,1)S(1)}, bf16[1024,576]{0,1:T(8,128)(2,1)}, u32[]{:S(2)}) copy-start(bf16[1024,576]{0,1:T(8,128)(2,1)} %all-gather.2.cloned.1.call-done) | copy-start | bytes 3538948
Sparse Core Ops, SparseCore 0:
  16.3 17.9 all-gather.1
  40.4 21.7 reduce-scatter.1
where the time goes:
time: 69.4 us; the launch traced here: 69 us
  waiting for transfers between devices  26.2 us (38%)
  blocking collectives  17 us (24%)
  between operations  14.2 us (20%)
  local copies, waits for them, and re-layouts  5.28 us (8%)
  matrix products  5.01 us (7%)
  other arithmetic  1.41 us (2%)
    reduce_scatter x1, waiting for transfers between devices, shards(): lax.psum_scatter(head_part.astype(jnp.bfloat16), 'head', scatter_dimensio...  21.9 us
    all_gather x1, blocking collectives, shards(): group_rows = lax.all_gather(cache, 'inner', axis=0, tiled=True)  9.6 us
    unnamed x1, blocking collectives  7.36 us
    all_gather x1, waiting for transfers between devices, shards(): segment = lax.all_gather(group_rows, 'outer', axis=0, tiled=True)  4.24 us
    unnamed x12, local copies, waits for them, and re-layouts  3.8 us
    dot_general x1, matrix products, one_block(): lax.dot_general(queries, key_block, (((1,), (1,)), ((), ())), preferred_e...  2.38 us
  transfers between devices with their start and end apart: 2, of which 2 were waited for; matrix products, arithmetic and copies ran while one was open for 8% of the time, Pallas kernels for 0%

commit v1 on v0

v1 whole, which is shorter than its diff:
```python
import functools

import jax
import jax.numpy as jnp
from jax import lax
from jax.experimental import pallas as pl
from jax.experimental.pallas import tpu as pltpu
from jax.sharding import PartitionSpec as P

LATENT = 512
ROPE = 64
NOPE = 128
VDIM = 128
SPAN = 64
TAG = 16

lowest_start = -1e30
log2e = 1.4426950408889634
soft_scale = (NOPE + ROPE) ** (-0.5)
VMEM_BYTES = 24 * 1024 * 1024
NT = (((1,), (1,)), ((), ()))
TOKENS = ("outer", "inner")


def vmem():
    return pl.BlockSpec(memory_space=pltpu.VMEM)


def smem():
    return pl.BlockSpec(memory_space=pltpu.SMEM)


def call(body, out_shape, n_scalar, args, flops, scratch=()):
    return pl.pallas_call(
        body,
        out_shape=out_shape,
        in_specs=[smem()] * n_scalar + [vmem()] * (len(args) - n_scalar),
        out_specs=jax.tree.map(lambda _: vmem(), out_shape),
        scratch_shapes=list(scratch),
        compiler_params=pltpu.CompilerParams(vmem_limit_bytes=VMEM_BYTES),
        cost_estimate=pl.CostEstimate(flops=flops, bytes_accessed=1 << 20, transcendentals=0),
    )(*args)


def build_queries(heads, nope_ref, rope_ref, key_up_ref, out_ref):
    rows = nope_ref.shape[0]
    for h in range(heads):
        here = slice(h * rows, (h + 1) * rows)
        latent = lax.dot_general(
            nope_ref[:, h * NOPE : (h + 1) * NOPE],
            key_up_ref[:, h * NOPE : (h + 1) * NOPE],
            NT,
            preferred_element_type=jnp.float32,
        )
        out_ref[here, :LATENT] = latent.astype(jnp.bfloat16)
        out_ref[here, LATENT : LATENT + ROPE] = rope_ref[:, h * ROPE : (h + 1) * ROPE]


def gather_keys(shards, keys):
    at = 0
    for ref in shards:
        keys[:, at : at + ref.shape[1]] = ref[...]
        at += ref.shape[1]


def positions(ids_ref, heads, rows):
    row = lax.broadcasted_iota(jnp.int32, (rows, 1), 0)
    pos = row % SPAN
    for k in range(rows // SPAN):
        pos = pos + jnp.where(row // SPAN == k, ids_ref[k] * SPAN, 0)
    return pos.astype(jnp.float32)


def scores_of(q, keys, row_pos):
    width = keys.shape[1]
    s = jnp.dot(q, keys[: LATENT + ROPE, :], preferred_element_type=jnp.float32)
    tag = keys[LATENT + ROPE : LATENT + ROPE + TAG, :][:1].astype(jnp.float32)
    lane = lax.broadcasted_iota(jnp.int32, (1, width), 1) % SPAN
    key_pos = tag * SPAN + lane.astype(jnp.float32)
    return jnp.where(key_pos <= row_pos, s, -jnp.inf)


def attend(heads, n_shards, first, ids_ref, q_ref, *refs):
    shards = refs[:n_shards]
    if first:
        m_ref, l_ref, acc_ref, keys = refs[n_shards:]
    else:
        m_in, l_in, acc_in, m_ref, l_ref, acc_ref, keys = refs[n_shards:]
    rows = q_ref.shape[0] // heads
    gather_keys(shards, keys)
    row_pos = positions(ids_ref, heads, rows)
    for h in range(heads):
        here = slice(h * rows, (h + 1) * rows)
        s = scores_of(q_ref[here, :], keys, row_pos)
        m = jnp.maximum(jnp.max(s, axis=1, keepdims=True), lowest_start)
        if not first:
            old = m_in[here, :1]
            m = jnp.maximum(m, old)
        w = jnp.exp2((s - m) * (soft_scale * log2e))
        l = jnp.sum(w, axis=1, keepdims=True)
        acc = lax.dot_general(
            w.astype(jnp.bfloat16), keys[:LATENT, :], NT, preferred_element_type=jnp.float32
        )
        if not first:
            again = jnp.exp2((old - m) * (soft_scale * log2e))
            l = l + l_in[here, :1] * again
            acc = acc + acc_in[here, :] * again
        m_ref[here, :] = jnp.broadcast_to(m, (rows, 128))
        l_ref[here, :] = jnp.broadcast_to(l, (rows, 128))
        acc_ref[here, :] = acc


def finish(heads, n_shards, parts, ids_ref, where_ref, q_ref, *refs):
    shards = refs[:n_shards]
    m_in, l_in, acc_in, value_ref, proj_ref = refs[n_shards : n_shards + 5]
    outs = refs[n_shards + 5 : n_shards + 5 + parts]
    keys, head_out = refs[n_shards + 5 + parts :]
    rows = q_ref.shape[0] // heads
    gather_keys(shards, keys)
    row_pos = positions(ids_ref, heads, rows)
    for h in range(heads):
        here = slice(h * rows, (h + 1) * rows)
        s = scores_of(q_ref[here, :], keys, row_pos)
        old = m_in[here, :1]
        m = jnp.maximum(jnp.max(s, axis=1, keepdims=True), old)
        w = jnp.exp2((s - m) * (soft_scale * log2e))
        again = jnp.exp2((old - m) * (soft_scale * log2e))
        l = jnp.sum(w, axis=1, keepdims=True) + l_in[here, :1] * again
        acc = lax.dot_general(
            w.astype(jnp.bfloat16), keys[:LATENT, :], NT, preferred_element_type=jnp.float32
        )
        latent = ((acc + acc_in[here, :] * again) / l).astype(jnp.bfloat16)
        head_out[:, h * VDIM : (h + 1) * VDIM] = jnp.dot(
            latent, value_ref[:, h * VDIM : (h + 1) * VDIM], preferred_element_type=jnp.float32
        ).astype(jnp.bfloat16)
    width = proj_ref.shape[1] // parts
    for k in range(parts):
        at = pl.multiple_of(where_ref[k] * width, 128)
        outs[k][...] = jnp.dot(
            head_out[...], proj_ref[:, pl.ds(at, width)], preferred_element_type=jnp.float32
        ).astype(outs[k].dtype)


def add_parts(*refs):
    total = refs[0][...].astype(jnp.float32)
    for ref in refs[1:-1]:
        total = total + ref[...].astype(jnp.float32)
    refs[-1][...] = total.astype(jnp.bfloat16)


def swap(a, axes, n, flip):
    return lax.ppermute(a, axes, [(i, flip(i)) for i in range(n)])


def shards(sizes, query_nope, query_rope, cache, span_ids, key_up, value_up, out_proj):
    head_n, outer_n, inner_n = sizes
    rows = cache.shape[0]
    heads = key_up.shape[1] // NOPE
    total_rows = heads * rows
    f32 = jnp.float32
    width = LATENT + ROPE + TAG
    tag = jnp.broadcast_to(
        jnp.repeat(span_ids, SPAN, total_repeat_length=rows)[None, :], (TAG, rows)
    ).astype(jnp.bfloat16)
    own = jnp.concatenate([cache.T, tag], axis=0)
    n = outer_n * inner_n
    core, step = inner_n, 2 * inner_n
    state_shape = (
        jax.ShapeDtypeStruct((total_rows, 128), f32),
        jax.ShapeDtypeStruct((total_rows, 128), f32),
        jax.ShapeDtypeStruct((total_rows, LATENT), f32),
    )

    queries = call(
        functools.partial(build_queries, heads),
        jax.ShapeDtypeStruct((total_rows, LATENT + ROPE), jnp.bfloat16),
        0,
        (query_nope, query_rope, key_up),
        2 * rows * NOPE * LATENT * heads,
    )

    def more(early, state):
        keys = sum(s.shape[1] for s in early)
        return call(
            functools.partial(attend, heads, len(early), state is None),
            state_shape,
            1,
            (span_ids, queries, *early) + (() if state is None else state),
            2 * total_rows * keys * (2 * LATENT + ROPE),
            [pltpu.VMEM((width, keys), jnp.bfloat16)],
        )

    if (outer_n, inner_n) == (4, 2):
        odd = lambda i: i & core
        near = lambda i: i ^ (1 if odd(i) else step)
        far = lambda i: i ^ (step if odd(i) else 1)
        pair = lambda a: swap(a, TOKENS, n, lambda i: i ^ core)
        first = swap(own, TOKENS, n, near)
        second = swap(own, TOKENS, n, far)
        third = swap(own, TOKENS, n, lambda i: i ^ (step + 1))
        early = [own, pair(own), first, second, pair(first), pair(second)]
        late = [third, pair(third)]
        state = more(early, None)
    else:
        everything = lax.all_gather(own, TOKENS, axis=1, tiled=True)
        chunk = 8 * rows
        blocks = everything.shape[1] // chunk
        piece = lambda i: lax.dynamic_slice_in_dim(everything, i * chunk, chunk, 1)
        state = lax.fori_loop(1, blocks, lambda i, s: more([piece(i)], s), more([piece(0)], None))
        late = [everything[:, (n - 1) * rows :]]
        if blocks == 1:
            raise NotImplementedError("one block")
    me = lax.axis_index("head")
    where = me ^ jnp.arange(head_n, dtype=jnp.int32)
    block = jax.ShapeDtypeStruct((rows, out_proj.shape[1] // head_n), jnp.bfloat16)
    keys = sum(s.shape[1] for s in late)
    parts = call(
        functools.partial(finish, heads, len(late), head_n),
        tuple(block for _ in range(head_n)),
        2,
        (span_ids, where, queries, *late, *state, value_up, out_proj),
        2 * total_rows * keys * (2 * LATENT + ROPE),
        [pltpu.VMEM((width, keys), jnp.bfloat16), pltpu.VMEM((rows, heads * VDIM), jnp.bfloat16)],
    )
    arrived = [
        swap(parts[k], "head", head_n, lambda i: i ^ k) for k in range(head_n - 1, 0, -1)
    ]
    return call(add_parts, block, 0, (parts[0], *arrived), 1 << 18)


def solution(mesh):
    sizes = tuple(mesh.shape[a] for a in ("head", "outer", "inner"))
    return jax.shard_map(
        functools.partial(shards, sizes),
        mesh=mesh,
        in_specs=(
            P(("outer", "inner"), "head"),
            P(("outer", "inner"), "head"),
            P(("outer", "inner"), None),
            P(("outer", "inner")),
            P(None, "head"),
            P(None, "head"),
            P("head", None),
        ),
        out_specs=P(("outer", "inner"), "head"),
        check_vma=False,
    )
```

time: 69.4 us -> 40.2 us (0.58)
  blocking collectives: 17 us -> 0 us
  between operations: 14.2 us -> 0.09 us
  waiting for transfers between devices: 26.2 us -> 15.1 us
  starting transfers between devices: 0.04 us -> 9.6 us
  Pallas kernels: 0 us -> 7.42 us
  matrix products: 5.01 us -> 0 us
  other arithmetic: 1.41 us -> 2.92 us
    reduce_scatter x1 -> x0, waiting for transfers between devices: 21.9 us -> none  [shards(): lax.psum_scatter(head_part.astype(jnp.bfloat16), 'head', scatter_dimensio...]
    ppermute x0 -> x10, waiting for transfers between devices: none -> 15.1 us  [swap(): return lax.ppermute(a, axes, [(i, flip(i)) for i in range(n)])]
    ppermute x0 -> x10, starting transfers between devices: none -> 9.6 us  [swap(): return lax.ppermute(a, axes, [(i, flip(i)) for i in range(n)])]
    all_gather x1 -> x0, blocking collectives: 9.6 us -> none  [shards(): group_rows = lax.all_gather(cache, 'inner', axis=0, tiled=True)]
    pallas_call x0 -> x4, Pallas kernels: none -> 7.42 us  [call(): pl.pallas_call(body, out_shape=out_shape, in_specs=[smem()] * n_scalar +...]
    unnamed x1 -> x0, blocking collectives: 7.36 us -> none
    dot_general x5 -> x0, matrix products: 5.01 us -> none  [the longest x1 2.38 us: one_block(): lax.dot_general(queries, key_block, (((1,), (1,)), ((), ())), preferred_e...]
    all_gather x1 -> x0, waiting for transfers between devices: 4.24 us -> none  [shards(): segment = lax.all_gather(group_rows, 'outer', axis=0, tiled=True)]
  transfers between devices with their start and end apart: 2 -> 10, of which waited for: 2 -> 4; matrix products, arithmetic and copies ran while one was open for 8% -> 0% of each run, Pallas kernels for 0% -> 9%
where the time goes in v1:
time: 40.2 us; the launch traced here: 39.9 us
  waiting for transfers between devices  15.1 us (38%)
  starting transfers between devices  9.6 us (24%)
  Pallas kernels  7.42 us (18%)
  local copies, waits for them, and re-layouts  4.77 us (12%)
  other arithmetic  2.92 us (7%)
    ppermute x10, waiting for transfers between devices, swap(): return lax.ppermute(a, axes, [(i, flip(i)) for i in range(n)])  15.1 us
    ppermute x10, starting transfers between devices, swap(): return lax.ppermute(a, axes, [(i, flip(i)) for i in range(n)])  9.6 us
    pallas_call x4, Pallas kernels, call(): pl.pallas_call(body, out_shape=out_shape, in_specs=[smem()] * n_scalar +...  7.42 us
    unnamed x12, local copies, waits for them, and re-layouts  3.44 us
    convert_element_type x1, other arithmetic, shards(): tag = jnp.broadcast_to(jnp.repeat(span_ids, SPAN, total_repeat_length=row...  1.99 us
    gather x1, local copies, waits for them, and re-layouts, shards(): jnp.repeat(span_ids, SPAN, total_repeat_length=rows)[None, :]  1.32 us
    concatenate x1, other arithmetic, shards(): own = jnp.concatenate([cache.T, tag], axis=0)  0.92 us
  transfers between devices with their start and end apart: 10, of which 4 were waited for; matrix products, arithmetic and copies ran while one was open for 0% of the time, Pallas kernels for 9%

profile of v1, /device:TPU:0, one launch (start us, length us, event | category | flops | bytes accessed | tf_op | source)
XLA Modules:
  0.0 39.9 jit_solution(14171083037338796498)
XLA Ops:
  0.0 1.3 %fusion = (s32[1]{0:T(128)}, s32[1]{0:T(128)}) fusion(s32[2]{0:T(128)} %ids_ref.3), kind=kLoop, calls=%fused_computation.3 | loop fusion | bytes 16 | tf_op jit(solution)/shard_map/jit(_take)/gather | solution.py:163
  1.3 2.0 %select_convert_fusion = bf16[128]{0:T(256)(128)(2,1)S(1)} fusion(pred[128]{0:T(512)(128)(4,1)} %constant.87, s32[]{:T(128)} %bitcast.2, s32[]{:T(128)} %bitcast.1), kind=kLoop, calls=%fused_computation.1 | loop fusion | flops 256 | bytes 392 | tf_op jit(solution)/shard_map/convert_element_type | solution.py:164
  3.3 0.9 %pad_maximum_fusion.refs_0_ = bf16[592,128]{1,0:T(8,128)(2,1)S(1)} fusion(bf16[16,128]{1,0:T(8,128)(2,1)S(1)} %broadcast_in_dim.6, bf16[576,128]{1,0:T(8,128)(2,1)} %bitcast.3), kind=kLoop, calls=%fused_computation | loop fusion | flops 303104 | bytes 303104 | tf_op jit(solution)/shard_map/concatenate | solution.py:165
  4.2 3.0 %collective-permute-start.3 = (bf16[592,128]{1,0:T(8,128)(2,1)S(1)}, bf16[592,128]{1,0:T(8,128)(2,1)S(1)}, u32[]{:S(2)}, u32[]{:S(2)}) collective-permute-start(bf16[592,128]{1,0:T(8,128)(2,1)S(1)} %pad_maximum_fusion.refs_0_), channel_id=1, source_target_pairs={{0,4},{1,5},{2,3},{3,2},{4,0},{5,1},{6,7},{7,6},{8,12},{9,13},{10,... | collective-permute-start | bytes 454664 | tf_op jit(solution)/shard_map/ppermute | solution.py:152
  7.3 1.5 %collective-permute-start.4 = (bf16[592,128]{1,0:T(8,128)(2,1)S(1)}, bf16[592,128]{1,0:T(8,128)(2,1)S(1)}, u32[]{:S(2)}, u32[]{:S(2)}) collective-permute-start(bf16[592,128]{1,0:T(8,128)(2,1)S(1)} %pad_maximum_fusion.refs_0_), channel_id=1, source_target_pairs={{0,1},{1,0},{2,6},{3,7},{4,5},{5,4},{6,2},{7,3},{8,9},{9,8},{10,14... | collective-permute-start | bytes 454664 | tf_op jit(solution)/shard_map/ppermute | solution.py:152
  8.8 0.0 collective-permute-start
  8.8 0.0 collective-permute-start.2
  8.8 2.7 %collective-permute-done.3.refs_2_ = bf16[592,128]{1,0:T(8,128)(2,1)S(1)} collective-permute-done((bf16[592,128]{1,0:T(8,128)(2,1)S(1)}, bf16[592,128]{1,0:T(8,128)(2,1)S(1)}, u32[]{:S(2)}, u32[]{:S(2)}) %collective-permute-start.3) | collective-permute-done | bytes 151584 | tf_op jit(solution)/shard_map/ppermute | solution.py:152
  11.5 3.3 %collective-permute-done.4.refs_3_ = bf16[592,128]{1,0:T(8,128)(2,1)S(1)} collective-permute-done((bf16[592,128]{1,0:T(8,128)(2,1)S(1)}, bf16[592,128]{1,0:T(8,128)(2,1)S(1)}, u32[]{:S(2)}, u32[]{:S(2)}) %collective-permute-start.4) | collective-permute-done | bytes 151584 | tf_op jit(solution)/shard_map/ppermute | solution.py:152
  14.8 0.0 collective-permute-start.6
  14.8 1.0 %copy-done.1 = bf16[512,512]{1,0:T(8,128)(2,1)S(1)} copy-done((bf16[512,512]{1,0:T(8,128)(2,1)S(1)}, bf16[512,512]{1,0:T(8,128)(2,1)}, u32[]{:S(2)}) %copy-start.1) | copy-done | bytes 524312
  15.8 0.9 %copy-done.3 = bf16[128,512]{1,0:T(8,128)(2,1)S(1)} copy-done((bf16[128,512]{1,0:T(8,128)(2,1)S(1)}, bf16[128,512]{1,0:T(8,128)(2,1)}, u32[]{:S(2)}) %copy-start.3) | copy-done | bytes 131096
  16.7 0.8 %copy-done.4 = bf16[128,256]{1,0:T(8,128)(2,1)S(1)} copy-done((bf16[128,256]{1,0:T(8,128)(2,1)S(1)}, bf16[128,256]{1,0:T(8,128)(2,1)}, u32[]{:S(2)}) %copy-start.4) | copy-done | bytes 65560
  17.6 0.3 shard_map.73.q_ref
  17.9 0.6 %collective-permute-start.1 = (bf16[592,128]{1,0:T(8,128)(2,1)S(1)}, bf16[592,128]{1,0:T(8,128)(2,1)S(1)}, u32[]{:S(2)}, u32[]{:S(2)}) collective-permute-start(bf16[592,128]{1,0:T(8,128)(2,1)S(1)} %collective-permute-done.refs_0_), channel_id=1, source_target_pairs={{0,2},{1,3},{2,0},{3,1},{4,6},{5,7},{6,4},{7,5},{8,10},{9,11},{10,... | collective-permute-start | bytes 454664 | tf_op jit(solution)/shard_map/ppermute | solution.py:152
  18.5 0.0 copy-start.5
  18.5 0.6 %copy-done.5 = s32[2]{0:T(128)S(1)} copy-done((s32[2]{0:T(128)S(1)}, s32[2]{0:T(128)}, u32[]{:S(2)}) %copy-start.5) | copy-done | bytes 32
  19.1 3.2 %shard_map.74 = (f32[512,128]{1,0:T(8,128)S(1)}, f32[512,128]{1,0:T(8,128)S(1)}, f32[512,512]{1,0:T(8,128)S(1)}) custom-call(s32[2]{0:T(128)S(1)} %copy-done.5, bf16[512,576]{1,0:T(8,128)(2,1)S(1)} %shard_map.73.q_ref, bf16[592,128]{1,0:T(8,128)(2,1)S(1)} %pad_maximum_fusion.refs_0_, bf16[592,128]{1,0:T(8,128)(2,1)S(1)} %collective-permute-done.2.refs_1_, ...), custom_call_target="tpu_custom_call" | custom-call | flops 855638016 | bytes 1048576 | tf_op jit(solution)/shard_map/pallas_call | solution.py:34
  22.4 3.2 %shard_map.75 = (bf16[128,512]{1,0:T(8,128)(2,1)S(1)}, bf16[128,512]{1,0:T(8,128)(2,1)S(1)}, bf16[128,512]{1,0:T(8,128)(2,1)S(1)}, bf16[128,512]{1,0:T(8,128)(2,1)S(1)}) custom-call(s32[2]{0:T(128)S(1)} %copy-done.5, s32[4]{0:T(128)S(1)} %iota_xor_fusion.where_ref, bf16[512,576]{1,0:T(8,128)(2,1)S(1)} %shard_map.73.q_ref, ...), custom_call_target="tpu_custom_call" | custom-call | flops 285212672 | bytes 1048576 | tf_op jit(solution)/shard_map/pallas_call | solution.py:34
  25.6 2.1 %collective-permute-start.7 = (bf16[128,512]{1,0:T(8,128)(2,1)S(1)}, bf16[128,512]{1,0:T(8,128)(2,1)S(1)}, u32[]{:S(2)}, u32[]{:S(2)}) collective-permute-start(bf16[128,512]{1,0:T(8,128)(2,1)S(1)} %get-tuple-element.28), channel_id=1, source_target_pairs={{0,24},{8,16},{16,8},{24,0},{1,25},{9,17},{17,9},{25,1},{2,26},{10... | collective-permute-start | bytes 393224 | tf_op jit(solution)/shard_map/ppermute | solution.py:152
  27.7 2.4 %collective-permute-start.9 = (bf16[128,512]{1,0:T(8,128)(2,1)S(1)}, bf16[128,512]{1,0:T(8,128)(2,1)S(1)}, u32[]{:S(2)}, u32[]{:S(2)}) collective-permute-start(bf16[128,512]{1,0:T(8,128)(2,1)S(1)} %get-tuple-element.30), channel_id=1, source_target_pairs={{0,8},{8,0},{16,24},{24,16},{1,9},{9,1},{17,25},{25,17},{2,10},{10... | collective-permute-start | bytes 393224 | tf_op jit(solution)/shard_map/ppermute | solution.py:152
  30.0 3.9 %collective-permute-done.7.refs_1_ = bf16[128,512]{1,0:T(8,128)(2,1)S(1)} collective-permute-done((bf16[128,512]{1,0:T(8,128)(2,1)S(1)}, bf16[128,512]{1,0:T(8,128)(2,1)S(1)}, u32[]{:S(2)}, u32[]{:S(2)}) %collective-permute-start.7) | collective-permute-done | bytes 131104 | tf_op jit(solution)/shard_map/ppermute | solution.py:152
  34.0 5.2 %collective-permute-done.8.refs_2_ = bf16[128,512]{1,0:T(8,128)(2,1)S(1)} collective-permute-done((bf16[128,512]{1,0:T(8,128)(2,1)S(1)}, bf16[128,512]{1,0:T(8,128)(2,1)S(1)}, u32[]{:S(2)}, u32[]{:S(2)}) %collective-permute-start.8) | collective-permute-done | bytes 131104 | tf_op jit(solution)/shard_map/ppermute | solution.py:152
  39.2 0.7 %shard_map.76 = bf16[128,512]{1,0:T(8,128)(2,1)} custom-call(bf16[128,512]{1,0:T(8,128)(2,1)S(1)} %get-tuple-element.27.refs_0_, bf16[128,512]{1,0:T(8,128)(2,1)S(1)} %collective-permute-done.7.refs_1_, bf16[128,512]{1,0:T(8,128)(2,1)S(1)} %collective-permute-done.8.refs_2_, bf16[128,512]{1,0:T(8,128)(2,1)S(1)} %collective-permute-done.9.refs_3_), custom_call_target="tpu_custom_call" | custom-call | flops 262144 | bytes 1048576 | tf_op jit(solution)/shard_map/pallas_call | solution.py:34
  (17 shorter events, 0.0 us)
Async XLA Ops:
  4.2 7.3 %collective-permute-start.3 = (bf16[592,128]{1,0:T(8,128)(2,1)S(1)}, bf16[592,128]{1,0:T(8,128)(2,1)S(1)}, u32[]{:S(2)}, u32[]{:S(2)}) collective-permute-start(bf16[592,128]{1,0:T(8,128)(2,1)S(1)} %pad_maximum_fusion.refs_0_), channel_id=1, source_target_pairs={{0,4},{1,5},{2,3},{3,2},{4,0},{5,1},{6,7},{7,6},{8,12},{9,13},{10,... | collective-permute-start | bytes 454664 | tf_op jit(solution)/shard_map/ppermute | solution.py:152
  7.3 7.5 %collective-permute-start.4 = (bf16[592,128]{1,0:T(8,128)(2,1)S(1)}, bf16[592,128]{1,0:T(8,128)(2,1)S(1)}, u32[]{:S(2)}, u32[]{:S(2)}) collective-permute-start(bf16[592,128]{1,0:T(8,128)(2,1)S(1)} %pad_maximum_fusion.refs_0_), channel_id=1, source_target_pairs={{0,1},{1,0},{2,6},{3,7},{4,5},{5,4},{6,2},{7,3},{8,9},{9,8},{10,14... | collective-permute-start | bytes 454664 | tf_op jit(solution)/shard_map/ppermute | solution.py:152
  8.8 9.1 %collective-permute-start = (bf16[592,128]{1,0:T(8,128)(2,1)S(1)}, bf16[592,128]{1,0:T(8,128)(2,1)S(1)}, u32[]{:S(2)}, u32[]{:S(2)}) collective-permute-start(bf16[592,128]{1,0:T(8,128)(2,1)S(1)} %pad_maximum_fusion.refs_0_), channel_id=1, source_target_pairs={{0,5},{1,4},{2,7},{3,6},{4,1},{5,0},{6,3},{7,2},{8,13},{9,12},{10,... | collective-permute-start | bytes 454664 | tf_op jit(solution)/shard_map/ppermute | solution.py:152
  8.8 9.7 %collective-permute-start.2 = (bf16[592,128]{1,0:T(8,128)(2,1)S(1)}, bf16[592,128]{1,0:T(8,128)(2,1)S(1)}, u32[]{:S(2)}, u32[]{:S(2)}) collective-permute-start(bf16[592,128]{1,0:T(8,128)(2,1)S(1)} %pad_maximum_fusion.refs_0_), channel_id=1, source_target_pairs={{0,2},{1,3},{2,0},{3,1},{4,6},{5,7},{6,4},{7,5},{8,10},{9,11},{10,... | collective-permute-start | bytes 454664 | tf_op jit(solution)/shard_map/ppermute | solution.py:152
  11.5 7.0 %collective-permute-start.5 = (bf16[592,128]{1,0:T(8,128)(2,1)S(1)}, bf16[592,128]{1,0:T(8,128)(2,1)S(1)}, u32[]{:S(2)}, u32[]{:S(2)}) collective-permute-start(bf16[592,128]{1,0:T(8,128)(2,1)S(1)} %collective-permute-done.3.refs_2_), channel_id=1, source_target_pairs={{0,2},{1,3},{2,0},{3,1},{4,6},{5,7},{6,4},{7,5},{8,10},{9,11},{10,... | collective-permute-start | bytes 454664 | tf_op jit(solution)/shard_map/ppermute | solution.py:152
  14.8 3.7 %collective-permute-start.6 = (bf16[592,128]{1,0:T(8,128)(2,1)S(1)}, bf16[592,128]{1,0:T(8,128)(2,1)S(1)}, u32[]{:S(2)}, u32[]{:S(2)}) collective-permute-start(bf16[592,128]{1,0:T(8,128)(2,1)S(1)} %collective-permute-done.4.refs_3_), channel_id=1, source_target_pairs={{0,2},{1,3},{2,0},{3,1},{4,6},{5,7},{6,4},{7,5},{8,10},{9,11},{10,... | collective-permute-start | bytes 454664 | tf_op jit(solution)/shard_map/ppermute | solution.py:152
  14.8 1.0 %copy-start.1 = (bf16[512,512]{1,0:T(8,128)(2,1)S(1)}, bf16[512,512]{1,0:T(8,128)(2,1)}, u32[]{:S(2)}) copy-start(bf16[512,512]{1,0:T(8,128)(2,1)} %key_up_ref.1) | copy-start | bytes 1572868
  15.8 0.9 %copy-start.3 = (bf16[128,512]{1,0:T(8,128)(2,1)S(1)}, bf16[128,512]{1,0:T(8,128)(2,1)}, u32[]{:S(2)}) copy-start(bf16[128,512]{1,0:T(8,128)(2,1)} %nope_ref.1) | copy-start | bytes 393220
  16.7 0.8 %copy-start.4 = (bf16[128,256]{1,0:T(8,128)(2,1)S(1)}, bf16[128,256]{1,0:T(8,128)(2,1)}, u32[]{:S(2)}) copy-start(bf16[128,256]{1,0:T(8,128)(2,1)} %rope_ref.1) | copy-start | bytes 196612
  17.6 4.8 %copy-start = (bf16[512,2048]{1,0:T(8,128)(2,1)S(1)}, bf16[512,2048]{1,0:T(8,128)(2,1)}, u32[]{:S(2)}) copy-start(bf16[512,2048]{1,0:T(8,128)(2,1)} %refs_6_.1) | copy-start | bytes 6291460
  17.6 4.8 %copy-start.2 = (bf16[512,512]{1,0:T(8,128)(2,1)S(1)}, bf16[512,512]{1,0:T(8,128)(2,1)}, u32[]{:S(2)}) copy-start(bf16[512,512]{1,0:T(8,128)(2,1)} %refs_5_.1) | copy-start | bytes 1572868
  17.9 4.5 %collective-permute-start.1 = (bf16[592,128]{1,0:T(8,128)(2,1)S(1)}, bf16[592,128]{1,0:T(8,128)(2,1)S(1)}, u32[]{:S(2)}, u32[]{:S(2)}) collective-permute-start(bf16[592,128]{1,0:T(8,128)(2,1)S(1)} %collective-permute-done.refs_0_), channel_id=1, source_target_pairs={{0,2},{1,3},{2,0},{3,1},{4,6},{5,7},{6,4},{7,5},{8,10},{9,11},{10,... | collective-permute-start | bytes 454664 | tf_op jit(solution)/shard_map/ppermute | solution.py:152
  18.5 0.7 %copy-start.5 = (s32[2]{0:T(128)S(1)}, s32[2]{0:T(128)}, u32[]{:S(2)}) copy-start(s32[2]{0:T(128)} %ids_ref.3) | copy-start | bytes 28
  25.6 8.4 %collective-permute-start.7 = (bf16[128,512]{1,0:T(8,128)(2,1)S(1)}, bf16[128,512]{1,0:T(8,128)(2,1)S(1)}, u32[]{:S(2)}, u32[]{:S(2)}) collective-permute-start(bf16[128,512]{1,0:T(8,128)(2,1)S(1)} %get-tuple-element.28), channel_id=1, source_target_pairs={{0,24},{8,16},{16,8},{24,0},{1,25},{9,17},{17,9},{25,1},{2,26},{10... | collective-permute-start | bytes 393224 | tf_op jit(solution)/shard_map/ppermute | solution.py:152
  27.7 11.5 %collective-permute-start.8 = (bf16[128,512]{1,0:T(8,128)(2,1)S(1)}, bf16[128,512]{1,0:T(8,128)(2,1)S(1)}, u32[]{:S(2)}, u32[]{:S(2)}) collective-permute-start(bf16[128,512]{1,0:T(8,128)(2,1)S(1)} %get-tuple-element.29), channel_id=1, source_target_pairs={{0,16},{8,24},{16,0},{24,8},{1,17},{9,25},{17,1},{25,9},{2,18},{10... | collective-permute-start | bytes 393224 | tf_op jit(solution)/shard_map/ppermute | solution.py:152
  27.7 11.5 %collective-permute-start.9 = (bf16[128,512]{1,0:T(8,128)(2,1)S(1)}, bf16[128,512]{1,0:T(8,128)(2,1)S(1)}, u32[]{:S(2)}, u32[]{:S(2)}) collective-permute-start(bf16[128,512]{1,0:T(8,128)(2,1)S(1)} %get-tuple-element.30), channel_id=1, source_target_pairs={{0,8},{8,0},{16,24},{24,16},{1,9},{9,1},{17,25},{25,17},{2,10},{10... | collective-permute-start | bytes 393224 | tf_op jit(solution)/shard_map/ppermute | solution.py:152

commit v2 on v1

v2 whole, which is shorter than its diff:
```python
import functools

import jax
import jax.numpy as jnp
from jax import lax
from jax.experimental import pallas as pl
from jax.experimental.pallas import tpu as pltpu
from jax.sharding import PartitionSpec as P


LATENT = 512
ROPE = 64
NOPE = 128
VDIM = 128
SPAN = 64
TAG = 16

lowest_start = -1e30
log2e = 1.4426950408889634
soft_scale = (NOPE + ROPE) ** (-0.5)
VMEM_BYTES = 24 * 1024 * 1024
NT = (((1,), (1,)), ((), ()))
TOKENS = ("outer", "inner")


def call(body, out_shape, args, flops, scratch=(), spaces=pltpu.VMEM):
    if spaces == pltpu.HBM:
        args = [pltpu.with_memory_space_constraint(a, pltpu.HBM) for a in args]
    return pl.pallas_call(
        body,
        out_shape=out_shape,
        in_specs=[pl.BlockSpec(memory_space=spaces)] * len(args),
        out_specs=jax.tree.map(lambda _: pl.BlockSpec(memory_space=pltpu.VMEM), out_shape),
        scratch_shapes=list(scratch),
        compiler_params=pltpu.CompilerParams(vmem_limit_bytes=VMEM_BYTES),
        cost_estimate=pl.CostEstimate(flops=flops, bytes_accessed=1 << 20, transcendentals=0),
    )(*args)


def prepare(ids_ref, cache_ref, out_ref, ids, sems):
    rows = cache_ref.shape[1]
    keys_in = pltpu.make_async_copy(cache_ref, out_ref.at[: LATENT + ROPE, :], sems.at[0])
    ids_in = pltpu.make_async_copy(ids_ref, ids, sems.at[1])
    keys_in.start()
    ids_in.start()
    ids_in.wait()
    lane = lax.broadcasted_iota(jnp.int32, (TAG, rows), 1)
    tag = jnp.zeros((TAG, rows), jnp.int32)
    for k in range(rows // SPAN):
        tag = jnp.where(lane // SPAN == k, ids[k], tag)
    out_ref[LATENT + ROPE :, :] = tag.astype(jnp.float32).astype(jnp.bfloat16)
    keys_in.wait()


def build_queries(heads, *refs):
    _, _, _, _, out_ref, pos_ref = refs[:6]
    key_up_ref, nope_ref, rope_ref, ids, sems = refs[6:]
    rows = nope_ref.shape[0]
    pairs = zip(refs[:4], refs[6:10])
    loads = [pltpu.make_async_copy(src, dst, sems.at[k]) for k, (src, dst) in enumerate(pairs)]
    for load in loads:
        load.start()
    for load in loads:
        load.wait()
    for h in range(heads):
        here = slice(h * rows, (h + 1) * rows)
        latent = lax.dot_general(
            nope_ref[:, h * NOPE : (h + 1) * NOPE],
            key_up_ref[:, h * NOPE : (h + 1) * NOPE],
            NT,
            preferred_element_type=jnp.float32,
        )
        out_ref[here, :LATENT] = latent.astype(jnp.bfloat16)
        out_ref[here, LATENT : LATENT + ROPE] = rope_ref[:, h * ROPE : (h + 1) * ROPE]
    row = lax.broadcasted_iota(jnp.int32, pos_ref.shape, 0) % rows
    pos = row % SPAN
    for k in range(rows // SPAN):
        pos = pos + jnp.where(row // SPAN == k, ids[k] * SPAN, 0)
    pos_ref[...] = pos.astype(jnp.float32)


def gather_keys(shards, keys):
    at = 0
    for ref in shards:
        keys[:, at : at + ref.shape[1]] = ref[...]
        at += ref.shape[1]


def scores_of(q_ref, pos_ref, keys):
    width = keys.shape[1]
    s = jnp.dot(q_ref[...], keys[: LATENT + ROPE, :], preferred_element_type=jnp.float32)
    tag = keys[LATENT + ROPE : LATENT + ROPE + TAG, :][:1].astype(jnp.float32)
    lane = lax.broadcasted_iota(jnp.int32, (1, width), 1) % SPAN
    key_pos = tag * SPAN + lane.astype(jnp.float32)
    return jnp.where(key_pos <= pos_ref[:, :1], s, -jnp.inf)


def weigh(s, m, keys):
    w = jnp.exp2((s - m) * (soft_scale * log2e))
    acc = lax.dot_general(
        w.astype(jnp.bfloat16), keys[:LATENT, :], NT, preferred_element_type=jnp.float32
    )
    return jnp.sum(w, axis=1, keepdims=True), acc


def attend(n_shards, first, q_ref, pos_ref, *refs):
    shards = refs[:n_shards]
    if first:
        m_ref, l_ref, acc_ref, keys = refs[n_shards:]
    else:
        m_in, l_in, acc_in, m_ref, l_ref, acc_ref, keys = refs[n_shards:]
    gather_keys(shards, keys)
    s = scores_of(q_ref, pos_ref, keys)
    old = lowest_start if first else m_in[:, :1]
    m = jnp.maximum(jnp.max(s, axis=1, keepdims=True), old)
    l, acc = weigh(s, m, keys)
    if not first:
        again = jnp.exp2((old - m) * (soft_scale * log2e))
        l = l + l_in[:, :1] * again
        acc = acc + acc_in[...] * again
    m_ref[...] = jnp.broadcast_to(m, m_ref.shape)
    l_ref[...] = jnp.broadcast_to(l, l_ref.shape)
    acc_ref[...] = acc


def finish(heads, n_shards, parts, q_ref, pos_ref, *refs):
    shards = refs[:n_shards]
    m_in, l_in, acc_in, value_ref, proj_ref = refs[n_shards : n_shards + 5]
    outs = refs[n_shards + 5 : n_shards + 5 + parts]
    keys, head_out = refs[n_shards + 5 + parts :]
    rows = q_ref.shape[0] // heads
    gather_keys(shards, keys)
    s = scores_of(q_ref, pos_ref, keys)
    old = m_in[:, :1]
    m = jnp.maximum(jnp.max(s, axis=1, keepdims=True), old)
    l, acc = weigh(s, m, keys)
    again = jnp.exp2((old - m) * (soft_scale * log2e))
    l = l + l_in[:, :1] * again
    latent = ((acc + acc_in[...] * again) * (1.0 / l)).astype(jnp.bfloat16)
    for h in range(heads):
        head_out[:, h * VDIM : (h + 1) * VDIM] = jnp.dot(
            latent[h * rows : (h + 1) * rows],
            value_ref[:, h * VDIM : (h + 1) * VDIM],
            preferred_element_type=jnp.float32,
        ).astype(jnp.bfloat16)
    width = proj_ref.shape[1] // parts
    me = lax.axis_index("head")
    odd = lax.axis_index("outer") % 2
    flips = [(0, 0), (3, 1), (1, 3), (2, 2)] if parts == 4 else [(k, k) for k in range(parts)]
    for out, (even_flip, odd_flip) in zip(outs, flips):
        dest = me ^ (even_flip + odd * (odd_flip - even_flip))
        at = pl.multiple_of(dest * width, 128)
        out[...] = jnp.dot(
            head_out[...], proj_ref[:, pl.ds(at, width)], preferred_element_type=jnp.float32
        ).astype(out.dtype)


def add_parts(*refs):
    total = refs[0][...].astype(jnp.float32)
    for ref in refs[1:-1]:
        total = total + ref[...].astype(jnp.float32)
    refs[-1][...] = total.astype(jnp.bfloat16)


def swap(a, axes, n, flip):
    return lax.ppermute(a, axes, [(i, flip(i)) for i in range(n)])


def shards(sizes, query_nope, query_rope, cache, span_ids, key_up, value_up, out_proj):
    head_n, outer_n, inner_n = sizes
    rows = cache.shape[0]
    heads = key_up.shape[1] // NOPE
    total_rows = heads * rows
    bf16, f32 = jnp.bfloat16, jnp.float32
    width = LATENT + ROPE + TAG
    n = outer_n * inner_n
    core, step = inner_n, 2 * inner_n
    state_shape = (
        jax.ShapeDtypeStruct((total_rows, 128), f32),
        jax.ShapeDtypeStruct((total_rows, 128), f32),
        jax.ShapeDtypeStruct((total_rows, LATENT), f32),
    )
    own = call(
        prepare,
        jax.ShapeDtypeStruct((width, rows), bf16),
        (span_ids, cache.T),
        1 << 20,
        [pltpu.SMEM(span_ids.shape, jnp.int32), pltpu.SemaphoreType.DMA((2,))],
        pltpu.HBM,
    )
    queries, row_pos = call(
        functools.partial(build_queries, heads),
        (
            jax.ShapeDtypeStruct((total_rows, LATENT + ROPE), bf16),
            jax.ShapeDtypeStruct((total_rows, 128), f32),
        ),
        (key_up, query_nope, query_rope, span_ids),
        2 * rows * NOPE * LATENT * heads,
        [pltpu.VMEM(a.shape, a.dtype) for a in (key_up, query_nope, query_rope)]
        + [pltpu.SMEM(span_ids.shape, jnp.int32), pltpu.SemaphoreType.DMA((4,))],
        pltpu.HBM,
    )

    def more(early, state):
        keys = sum(s.shape[1] for s in early)
        return call(
            functools.partial(attend, len(early), state is None),
            state_shape,
            (queries, row_pos, *early) + (() if state is None else tuple(state)),
            2 * total_rows * keys * (2 * LATENT + ROPE),
            [pltpu.VMEM((width, keys), bf16)],
        )

    if (outer_n, inner_n) == (4, 2):
        odd = lambda i: i & core
        near = lambda i: i ^ (1 if odd(i) else step)
        far = lambda i: i ^ (step if odd(i) else 1)
        pair = lambda a: swap(a, TOKENS, n, lambda i: i ^ core)
        first = swap(own, TOKENS, n, near)
        second = swap(own, TOKENS, n, far)
        third = swap(own, TOKENS, n, lambda i: i ^ (step + 1))
        other = pair(own)
        first_pair = pair(first)
        state = more([own, other, first, first_pair], None)
        late = [second, third, pair(second), pair(third)]
    else:
        everything = lax.all_gather(own, TOKENS, axis=1, tiled=True)
        chunk = 8 * rows
        piece = lambda i: lax.dynamic_slice_in_dim(everything, i * chunk, chunk, 1)
        state = more([piece(0)], None)
        last = n // 8 - 1
        state = lax.fori_loop(1, last, lambda i, s: more([piece(i)], s), state)
        late = [everything[:, last * chunk :]]
    block = jax.ShapeDtypeStruct((rows, out_proj.shape[1] // head_n), bf16)
    keys = sum(s.shape[1] for s in late)
    parts = call(
        functools.partial(finish, heads, len(late), head_n),
        tuple(block for _ in range(head_n)),
        (queries, row_pos, *late, *state, value_up, out_proj),
        2 * total_rows * keys * (2 * LATENT + ROPE),
        [pltpu.VMEM((width, keys), bf16), pltpu.VMEM((rows, heads * VDIM), bf16)],
    )
    if head_n == 4:
        mesh_axes = ("head", "outer", "inner")

        def ring(a, even_flip, odd_flip):
            def to(i):
                odd = (i // inner_n) % 2
                return i ^ ((odd_flip if odd else even_flip) * n)

            return swap(a, mesh_axes, head_n * n, to)

        relayed = ring(parts[3], 3, 1)
        straight = ring(parts[1], 3, 1)
        onward = ring((parts[2].astype(f32) + relayed.astype(f32)).astype(bf16), 1, 3)
        arrived = [straight, onward]
    else:
        arrived = [swap(parts[k], "head", head_n, lambda i: i ^ k) for k in range(1, head_n)]
    return call(add_parts, block, (parts[0], *arrived), 1 << 18)


def solution(mesh):
    sizes = tuple(mesh.shape[a] for a in ("head", "outer", "inner"))

    def body(*args):
        return shards(sizes, *args)

    return jax.shard_map(
        body,
        mesh=mesh,
        in_specs=(
            P(("outer", "inner"), "head"),
            P(("outer", "inner"), "head"),
            P(("outer", "inner"), None),
            P(("outer", "inner")),
            P(None, "head"),
            P(None, "head"),
            P("head", None),
        ),
        out_specs=P(("outer", "inner"), "head"),
        check_vma=False,
    )
```

time: 40.2 us -> 31.9 us (0.79)
  local copies, waits for them, and re-layouts: 4.77 us -> 0.01 us
  other arithmetic: 2.92 us -> 0.03 us
  waiting for transfers between devices: 15.1 us -> 16.8 us
  Pallas kernels: 7.42 us -> 6.26 us
  starting transfers between devices: 9.6 us -> 8.55 us
    unnamed x12 -> x4, local copies, waits for them, and re-layouts: 3.44 us -> 0.01 us
    convert_element_type x1, other arithmetic: 1.99 us -> 0.03 us  [shards(): (parts[2].astype(f32) + relayed.astype(f32)).astype(bf16)]
    ppermute x10, waiting for transfers between devices: 15.1 us -> 16.8 us  [swap(): return lax.ppermute(a, axes, [(i, flip(i)) for i in range(n)])]
    gather x1 -> x0, local copies, waits for them, and re-layouts: 1.32 us -> none  [shards(): jnp.repeat(span_ids, SPAN, total_repeat_length=rows)[None, :]]
    pallas_call x4 -> x5, Pallas kernels: 7.42 us -> 6.26 us  [call(): pl.pallas_call(body, out_shape=out_shape, in_specs=[pl.BlockSpec(memory_s...]
    ppermute x10, starting transfers between devices: 9.6 us -> 8.55 us  [swap(): return lax.ppermute(a, axes, [(i, flip(i)) for i in range(n)])]
    concatenate x1 -> x0, other arithmetic: 0.92 us -> none  [shards(): own = jnp.concatenate([cache.T, tag], axis=0)]
  transfers between devices with their start and end apart: 10 -> 10, of which waited for: 4 -> 6; matrix products, arithmetic and copies ran while one was open for 0% -> 0% of each run, Pallas kernels for 9% -> 8%
where the time goes in v2:
time: 31.9 us; the launch traced here: 31.7 us
  waiting for transfers between devices  16.8 us (53%)
  starting transfers between devices  8.55 us (27%)
  Pallas kernels  6.26 us (20%)
    ppermute x10, waiting for transfers between devices, swap(): return lax.ppermute(a, axes, [(i, flip(i)) for i in range(n)])  16.8 us
    ppermute x10, starting transfers between devices, swap(): return lax.ppermute(a, axes, [(i, flip(i)) for i in range(n)])  8.55 us
    pallas_call x5, Pallas kernels, call(): pl.pallas_call(body, out_shape=out_shape, in_specs=[pl.BlockSpec(memory_s...  6.26 us
  transfers between devices with their start and end apart: 10, of which 6 were waited for; matrix products, arithmetic and copies ran while one was open for 0% of the time, Pallas kernels for 8%

profile of v2, /device:TPU:0, one launch (start us, length us, event | category | flops | bytes accessed | tf_op | source)
XLA Modules:
  0.0 31.7 jit_solution(2559554892217663389)
XLA Ops:
  0.0 1.1 %shard_map.74.refs_0_ = bf16[592,128]{1,0:T(8,128)(2,1)S(1)} custom-call(s32[2]{0:T(128)} %ids_ref.1, bf16[576,128]{1,0:T(8,128)(2,1)} %bitcast.1), custom_call_target="tpu_custom_call" | custom-call | flops 1048576 | bytes 1048576 | tf_op jit(solution)/shard_map/pallas_call | solution.py:29
  1.1 3.0 %collective-permute-start.5 = (bf16[592,128]{1,0:T(8,128)(2,1)S(1)}, bf16[592,128]{1,0:T(8,128)(2,1)S(1)}, u32[]{:S(2)}, u32[]{:S(2)}) collective-permute-start(bf16[592,128]{1,0:T(8,128)(2,1)S(1)} %shard_map.74.refs_0_), channel_id=1, source_target_pairs={{0,4},{1,5},{2,3},{3,2},{4,0},{5,1},{6,7},{7,6},{8,12},{9,13},{10,... | collective-permute-start | bytes 454664 | tf_op jit(solution)/shard_map/ppermute | solution.py:166
  4.1 1.5 %collective-permute-start = (bf16[592,128]{1,0:T(8,128)(2,1)S(1)}, bf16[592,128]{1,0:T(8,128)(2,1)S(1)}, u32[]{:S(2)}, u32[]{:S(2)}) collective-permute-start(bf16[592,128]{1,0:T(8,128)(2,1)S(1)} %shard_map.74.refs_0_), channel_id=1, source_target_pairs={{0,1},{1,0},{2,6},{3,7},{4,5},{5,4},{6,2},{7,3},{8,9},{9,8},{10,14... | collective-permute-start | bytes 454664 | tf_op jit(solution)/shard_map/ppermute | solution.py:166
  5.6 0.0 collective-permute-start.1
  5.7 0.0 collective-permute-start.4
  5.7 2.7 %collective-permute-done.5.refs_2_ = bf16[592,128]{1,0:T(8,128)(2,1)S(1)} collective-permute-done((bf16[592,128]{1,0:T(8,128)(2,1)S(1)}, bf16[592,128]{1,0:T(8,128)(2,1)S(1)}, u32[]{:S(2)}, u32[]{:S(2)}) %collective-permute-start.5) | collective-permute-done | bytes 151584 | tf_op jit(solution)/shard_map/ppermute | solution.py:166
  8.3 0.0 collective-permute-start.6
  8.3 3.3 %collective-permute-done.refs_0_ = bf16[592,128]{1,0:T(8,128)(2,1)S(1)} collective-permute-done((bf16[592,128]{1,0:T(8,128)(2,1)S(1)}, bf16[592,128]{1,0:T(8,128)(2,1)S(1)}, u32[]{:S(2)}, u32[]{:S(2)}) %collective-permute-start) | collective-permute-done | bytes 151584 | tf_op jit(solution)/shard_map/ppermute | solution.py:166
  11.6 0.0 collective-permute-start.2
  11.6 1.0 %collective-permute-done.1.refs_1_ = bf16[592,128]{1,0:T(8,128)(2,1)S(1)} collective-permute-done((bf16[592,128]{1,0:T(8,128)(2,1)S(1)}, bf16[592,128]{1,0:T(8,128)(2,1)S(1)}, u32[]{:S(2)}, u32[]{:S(2)}) %collective-permute-start.1) | collective-permute-done | bytes 151584 | tf_op jit(solution)/shard_map/ppermute | solution.py:166
  12.6 0.0 collective-permute-start.3
  12.6 1.4 %shard_map.73 = (bf16[512,576]{1,0:T(8,128)(2,1)S(1)}, f32[512,128]{1,0:T(8,128)S(1)}) custom-call(bf16[512,512]{1,0:T(8,128)(2,1)} %refs_0_.1, bf16[128,512]{1,0:T(8,128)(2,1)} %refs_1_.1, bf16[128,256]{1,0:T(8,128)(2,1)} %refs_2_.1, s32[2]{0:T(128)} %ids_ref.1), custom_call_target="tpu_custom_call" | custom-call | flops 67108864 | bytes 1048576 | tf_op jit(solution)/shard_map/pallas_call | solution.py:29
  14.0 0.0 collective-permute-done.4.refs_1_
  14.0 1.2 %shard_map.75 = (f32[512,128]{1,0:T(8,128)S(1)}, f32[512,128]{1,0:T(8,128)S(1)}, f32[512,512]{1,0:T(8,128)S(1)}) custom-call(bf16[512,576]{1,0:T(8,128)(2,1)S(1)} %get-tuple-element.14.q_ref, f32[512,128]{1,0:T(8,128)S(1)} %get-tuple-element.15.pos_ref, bf16[592,128]{1,0:T(8,128)(2,1)S(1)} %shard_map.74.refs_0_, ...), custom_call_target="tpu_custom_call" | custom-call | flops 570425344 | bytes 1048576 | tf_op jit(solution)/shard_map/pallas_call | solution.py:29
  15.2 0.0 collective-permute-done.2.refs_2_
  15.2 0.0 collective-permute-done.3.refs_3_
  15.3 1.9 %shard_map.76 = (bf16[128,512]{1,0:T(8,128)(2,1)S(1)}, bf16[128,512]{1,0:T(8,128)(2,1)S(1)}, bf16[128,512]{1,0:T(8,128)(2,1)S(1)}, bf16[128,512]{1,0:T(8,128)(2,1)S(1)}) custom-call(bf16[512,576]{1,0:T(8,128)(2,1)S(1)} %get-tuple-element.14.q_ref, f32[512,128]{1,0:T(8,128)S(1)} %get-tuple-element.15.pos_ref, ...), custom_call_target="tpu_custom_call" | custom-call | flops 570425344 | bytes 1048576 | tf_op jit(solution)/shard_map/pallas_call | solution.py:29
  17.2 3.8 %collective-permute-start.8 = (bf16[128,512]{1,0:T(8,128)(2,1)S(1)}, bf16[128,512]{1,0:T(8,128)(2,1)S(1)}, u32[]{:S(2)}, u32[]{:S(2)}) collective-permute-start(bf16[128,512]{1,0:T(8,128)(2,1)S(1)} %get-tuple-element.22), channel_id=1, source_target_pairs={{0,24},{1,25},{2,10},{3,11},{4,28},{5,29},{6,14},{7,15},{8,16},{9,... | collective-permute-start | bytes 393224 | tf_op jit(solution)/shard_map/ppermute | solution.py:166
  21.0 0.1 collective-permute-start.7
  21.0 4.3 %collective-permute-done.8 = bf16[128,512]{1,0:T(8,128)(2,1)S(1)} collective-permute-done((bf16[128,512]{1,0:T(8,128)(2,1)S(1)}, bf16[128,512]{1,0:T(8,128)(2,1)S(1)}, u32[]{:S(2)}, u32[]{:S(2)}) %collective-permute-start.8) | collective-permute-done | bytes 131104 | tf_op jit(solution)/shard_map/ppermute | solution.py:166
  25.4 0.1 collective-permute-start.9
  25.5 3.7 %collective-permute-done.7.refs_1_ = bf16[128,512]{1,0:T(8,128)(2,1)S(1)} collective-permute-done((bf16[128,512]{1,0:T(8,128)(2,1)S(1)}, bf16[128,512]{1,0:T(8,128)(2,1)S(1)}, u32[]{:S(2)}, u32[]{:S(2)}) %collective-permute-start.7) | collective-permute-done | bytes 131104 | tf_op jit(solution)/shard_map/ppermute | solution.py:166
  29.3 1.8 %collective-permute-done.9.refs_2_ = bf16[128,512]{1,0:T(8,128)(2,1)S(1)} collective-permute-done((bf16[128,512]{1,0:T(8,128)(2,1)S(1)}, bf16[128,512]{1,0:T(8,128)(2,1)S(1)}, u32[]{:S(2)}, u32[]{:S(2)}) %collective-permute-start.9) | collective-permute-done | bytes 131104 | tf_op jit(solution)/shard_map/ppermute | solution.py:166
  31.0 0.7 %shard_map.77 = bf16[128,512]{1,0:T(8,128)(2,1)} custom-call(bf16[128,512]{1,0:T(8,128)(2,1)S(1)} %get-tuple-element.19.refs_0_, bf16[128,512]{1,0:T(8,128)(2,1)S(1)} %collective-permute-done.7.refs_1_, bf16[128,512]{1,0:T(8,128)(2,1)S(1)} %collective-permute-done.9.refs_2_), custom_call_target="tpu_custom_call" | custom-call | flops 262144 | bytes 1048576 | tf_op jit(solution)/shard_map/pallas_call | solution.py:29
  (6 shorter events, 0.0 us)
Async XLA Ops:
  0.0 15.2 %copy-start.1 = (bf16[512,512]{1,0:T(8,128)(2,1)S(1)}, bf16[512,512]{1,0:T(8,128)(2,1)}, u32[]{:S(2)}) copy-start(bf16[512,512]{1,0:T(8,128)(2,1)} %refs_7_.1) | copy-start | bytes 1572868
  0.0 15.2 %copy-start = (bf16[512,2048]{1,0:T(8,128)(2,1)S(1)}, bf16[512,2048]{1,0:T(8,128)(2,1)}, u32[]{:S(2)}) copy-start(bf16[512,2048]{1,0:T(8,128)(2,1)} %refs_8_.1) | copy-start | bytes 6291460
  1.1 7.3 %collective-permute-start.5 = (bf16[592,128]{1,0:T(8,128)(2,1)S(1)}, bf16[592,128]{1,0:T(8,128)(2,1)S(1)}, u32[]{:S(2)}, u32[]{:S(2)}) collective-permute-start(bf16[592,128]{1,0:T(8,128)(2,1)S(1)} %shard_map.74.refs_0_), channel_id=1, source_target_pairs={{0,4},{1,5},{2,3},{3,2},{4,0},{5,1},{6,7},{7,6},{8,12},{9,13},{10,... | collective-permute-start | bytes 454664 | tf_op jit(solution)/shard_map/ppermute | solution.py:166
  4.1 7.5 %collective-permute-start = (bf16[592,128]{1,0:T(8,128)(2,1)S(1)}, bf16[592,128]{1,0:T(8,128)(2,1)S(1)}, u32[]{:S(2)}, u32[]{:S(2)}) collective-permute-start(bf16[592,128]{1,0:T(8,128)(2,1)S(1)} %shard_map.74.refs_0_), channel_id=1, source_target_pairs={{0,1},{1,0},{2,6},{3,7},{4,5},{5,4},{6,2},{7,3},{8,9},{9,8},{10,14... | collective-permute-start | bytes 454664 | tf_op jit(solution)/shard_map/ppermute | solution.py:166
  5.6 6.9 %collective-permute-start.1 = (bf16[592,128]{1,0:T(8,128)(2,1)S(1)}, bf16[592,128]{1,0:T(8,128)(2,1)S(1)}, u32[]{:S(2)}, u32[]{:S(2)}) collective-permute-start(bf16[592,128]{1,0:T(8,128)(2,1)S(1)} %shard_map.74.refs_0_), channel_id=1, source_target_pairs={{0,5},{1,4},{2,7},{3,6},{4,1},{5,0},{6,3},{7,2},{8,13},{9,12},{10,... | collective-permute-start | bytes 454664 | tf_op jit(solution)/shard_map/ppermute | solution.py:166
  5.7 8.4 %collective-permute-start.4 = (bf16[592,128]{1,0:T(8,128)(2,1)S(1)}, bf16[592,128]{1,0:T(8,128)(2,1)S(1)}, u32[]{:S(2)}, u32[]{:S(2)}) collective-permute-start(bf16[592,128]{1,0:T(8,128)(2,1)S(1)} %shard_map.74.refs_0_), channel_id=1, source_target_pairs={{0,2},{1,3},{2,0},{3,1},{4,6},{5,7},{6,4},{7,5},{8,10},{9,11},{10,... | collective-permute-start | bytes 454664 | tf_op jit(solution)/shard_map/ppermute | solution.py:166
  8.3 5.7 %collective-permute-start.6 = (bf16[592,128]{1,0:T(8,128)(2,1)S(1)}, bf16[592,128]{1,0:T(8,128)(2,1)S(1)}, u32[]{:S(2)}, u32[]{:S(2)}) collective-permute-start(bf16[592,128]{1,0:T(8,128)(2,1)S(1)} %collective-permute-done.5.refs_2_), channel_id=1, source_target_pairs={{0,2},{1,3},{2,0},{3,1},{4,6},{5,7},{6,4},{7,5},{8,10},{9,11},{10,... | collective-permute-start | bytes 454664 | tf_op jit(solution)/shard_map/ppermute | solution.py:166
  11.6 3.6 %collective-permute-start.2 = (bf16[592,128]{1,0:T(8,128)(2,1)S(1)}, bf16[592,128]{1,0:T(8,128)(2,1)S(1)}, u32[]{:S(2)}, u32[]{:S(2)}) collective-permute-start(bf16[592,128]{1,0:T(8,128)(2,1)S(1)} %collective-permute-done.refs_0_), channel_id=1, source_target_pairs={{0,2},{1,3},{2,0},{3,1},{4,6},{5,7},{6,4},{7,5},{8,10},{9,11},{10,... | collective-permute-start | bytes 454664 | tf_op jit(solution)/shard_map/ppermute | solution.py:166
  12.6 2.6 %collective-permute-start.3 = (bf16[592,128]{1,0:T(8,128)(2,1)S(1)}, bf16[592,128]{1,0:T(8,128)(2,1)S(1)}, u32[]{:S(2)}, u32[]{:S(2)}) collective-permute-start(bf16[592,128]{1,0:T(8,128)(2,1)S(1)} %collective-permute-done.1.refs_1_), channel_id=1, source_target_pairs={{0,2},{1,3},{2,0},{3,1},{4,6},{5,7},{6,4},{7,5},{8,10},{9,11},{10,... | collective-permute-start | bytes 454664 | tf_op jit(solution)/shard_map/ppermute | solution.py:166
  17.2 8.2 %collective-permute-start.8 = (bf16[128,512]{1,0:T(8,128)(2,1)S(1)}, bf16[128,512]{1,0:T(8,128)(2,1)S(1)}, u32[]{:S(2)}, u32[]{:S(2)}) collective-permute-start(bf16[128,512]{1,0:T(8,128)(2,1)S(1)} %get-tuple-element.22), channel_id=1, source_target_pairs={{0,24},{1,25},{2,10},{3,11},{4,28},{5,29},{6,14},{7,15},{8,16},{9,... | collective-permute-start | bytes 393224 | tf_op jit(solution)/shard_map/ppermute | solution.py:166
  21.0 8.3 %collective-permute-start.7 = (bf16[128,512]{1,0:T(8,128)(2,1)S(1)}, bf16[128,512]{1,0:T(8,128)(2,1)S(1)}, u32[]{:S(2)}, u32[]{:S(2)}) collective-permute-start(bf16[128,512]{1,0:T(8,128)(2,1)S(1)} %get-tuple-element.20), channel_id=1, source_target_pairs={{0,24},{1,25},{2,10},{3,11},{4,28},{5,29},{6,14},{7,15},{8,16},{9,... | collective-permute-start | bytes 393224 | tf_op jit(solution)/shard_map/ppermute | solution.py:166
  25.4 5.6 %collective-permute-start.9 = (bf16[128,512]{1,0:T(8,128)(2,1)S(1)}, bf16[128,512]{1,0:T(8,128)(2,1)S(1)}, u32[]{:S(2)}, u32[]{:S(2)}) collective-permute-start(bf16[128,512]{1,0:T(8,128)(2,1)S(1)} %add_convert_fusion), channel_id=1, source_target_pairs={{0,8},{1,9},{2,26},{3,27},{4,12},{5,13},{6,30},{7,31},{8,0},{9,1},... | collective-permute-start | bytes 393224 | tf_op jit(solution)/shard_map/ppermute | solution.py:166
